TPU v7x, 128 devices: a whole 4x4x4 slice. The times are simulated.
128 devices in a mesh: layer: 8 (over x, z_hi), feat: 16 (over y, z_lo, core).
Axes of the slice: x: 4, y: 4, z: 4 (z_hi: 2, z_lo: 2; z = z_hi * 2 + z_lo), core: 2. Of those that a mesh axis runs over, the one named last changes fastest.
Arguments:
- residuals: bfloat16 [512, 4096], P('feat', 'layer'), may hold values from -6 to 6
- errors: bfloat16 [512, 4096], P('feat', 'layer'), may hold values from -0.26367188 to 0.26367188
- enc_weight: bfloat16 [4096, 65536], P('layer', 'feat'), may hold values from -0.09375 to 0.09375
- dec_weight: bfloat16 [4096, 65536], P('layer', 'feat'), may hold values from -0.09375 to 0.09375
- enc_bias: float32 [65536], P('feat'), may hold values from -3 to 3
Outputs:
- enc_grad: bfloat16 [4096, 65536], P('layer', 'feat')
- dec_grad: bfloat16 [4096, 65536], P('layer', 'feat')
- bias_grad: float32 [65536], P('feat')
All inputs are finite; a program needn't handle non-finite values.
Results may differ from a plain program's by a relative error of at most 0.0055.
Values may be sent and summed in bfloat16 or wider, within the bound.
A program may use at most 128 MiB of HBM per device.

v0:
```python
import jax
import jax.numpy as jnp
from jax import lax
from jax.sharding import PartitionSpec as P


def transposed(left, right):
    return lax.dot_general(
        left, right, (((0,), (0,)), ((), ())), preferred_element_type=jnp.float32
    )


def gate_values(preact, code_grad):
    code = (jax.nn.softplus(4.0 * preact) / 4.0).astype(jnp.bfloat16)
    masked = (code_grad * jax.nn.sigmoid(4.0 * preact)).astype(jnp.bfloat16)
    return (code, masked)


def per_device(residuals, errors, enc_weight, dec_weight, enc_bias):
    all_resid, all_errors = (
        lax.all_gather(residuals, "feat", axis=0, tiled=True),
        lax.all_gather(errors, "feat", axis=0, tiled=True),
    )
    resid_part = jnp.dot(all_resid, enc_weight, preferred_element_type=jnp.float32)
    error_part = jnp.dot(all_errors, dec_weight, preferred_element_type=jnp.float32)
    preact_sum, code_grad = lax.psum((resid_part, error_part), "layer")
    code, masked = gate_values(preact_sum + enc_bias, code_grad)
    enc_grad = transposed(all_resid, masked)
    dec_grad = transposed(all_errors, code)
    bias_grad = jnp.sum(masked.astype(jnp.float32), axis=0)
    return (enc_grad.astype(jnp.bfloat16), dec_grad.astype(jnp.bfloat16), bias_grad)


def solution(mesh):
    placed = (
        P("feat", "layer"),
        P("feat", "layer"),
        P("layer", "feat"),
        P("layer", "feat"),
        P("feat"),
    )
    return jax.shard_map(
        per_device,
        mesh=mesh,
        in_specs=placed,
        out_specs=(P("layer", "feat"), P("layer", "feat"), P("feat")),
        check_vma=False,
    )
```

profile of v0, /device:TPU:36, one launch (start us, length us, event | category | flops | bytes accessed | tf_op | source)
XLA Modules:
  0.0 764.3 jit_solution(3764518536659463589)
XLA Ops:
  7.2 0.0 all-reduce.3.cloned.1.call-start
  7.2 0.0 copy-start.2
  7.2 18.2 %all_gather.7 = bf16[512,512]{1,0:T(8,128)(2,1)S(1)} all-gather(bf16[32,512]{1,0:T(8,128)(2,1)} %param.5), channel_id=1, replica_groups=mesh['layer'=8,'feat'=16] {'feat'}, dimensions={0}, use_global_device_ids=true | all-gather | bytes 557056 | tf_op jit(solution)/shard_map/all_gather | solution.py:21
  25.4 21.7 %all_gather.6 = bf16[512,512]{1,0:T(8,128)(2,1)S(1)} all-gather(bf16[32,512]{1,0:T(8,128)(2,1)} %param.6), channel_id=1, replica_groups=mesh['layer'=8,'feat'=16] {'feat'}, dimensions={0}, use_global_device_ids=true | all-gather | bytes 557056 | tf_op jit(solution)/shard_map/all_gather | solution.py:22
  47.1 7.8 %fusion.8 = f32[512,4096]{1,0:T(8,128)} fusion(bf16[512,512]{1,0:T(8,128)(2,1)S(1)} %all_gather.6, bf16[512,4096]{1,0:T(8,128)(2,1)} %param.8), kind=kOutput, calls=%fused_computation.13 | convolution fusion | flops 2147483648 | bytes 13107200 | tf_op jit(solution)/shard_map/dot_general | solution.py:25
  54.9 0.0 copy-done.2
  54.9 5.6 fusion.9
  60.5 0.0 copy-start.3
  60.5 0.0 all-reduce.3.cloned.1.call-update
  60.6 660.6 %all-reduce.3.cloned.1.call-done = (f32[512,4096]{1,0:T(8,128)}, f32[512,4096]{1,0:T(8,128)}) async-done(((f32[512,4096]{1,0:T(8,128)}, f32[512,4096]{1,0:T(8,128)}), (f32[512,4096]{1,0:T(8,128)}, f32[512,4096]{1,0:T(8,128)})) %all-reduce.3.cloned.1.call-update) | async-done | bytes 16777232 | tf_op jit(solution)/shard_map/psum | solution.py:26
  721.1 0.0 copy-done.3
  721.1 0.0 copy-start
  721.1 0.0 copy-start.1
  721.1 12.6 %fusion.3 = bf16[512,4096]{0,1:T(8,128)(2,1)} fusion(bf16[512,512]{1,0:T(8,128)(2,1)S(1)} %all_gather.6, f32[512,4096]{1,0:T(8,128)} %get-tuple-element.7, f32[4096]{0:T(1024)S(1)} %copy-done.3), kind=kOutput, calls=%fused_computation.9 | convolution fusion | flops 2170552320 | bytes 13123584 | tf_op jit(solution)/shard_map/dot_general | solution.py:8
  733.7 0.0 copy-done
  733.7 0.0 copy-done.1
  733.7 4.6 convert_reduce_fusion
  738.3 6.3 copy.9
  744.6 6.5 fusion.2
  751.1 6.3 copy.8
Async XLA Ops:
  7.2 714.0 %all-reduce.3.cloned.1.call-start = ((), (), s32[]{:S(2)}) async-start(), calls=%async_computation | async-start | bytes 33554432 | tf_op jit(solution)/shard_map/psum | solution.py:26
  7.2 47.7 %copy-start.2 = (bf16[512,4096]{1,0:T(8,128)(2,1)S(1)}, bf16[512,4096]{1,0:T(8,128)(2,1)}, u32[]{:S(2)}) copy-start(bf16[512,4096]{1,0:T(8,128)(2,1)} %param.7) | copy-start | bytes 12582916
  60.5 660.6 %copy-start.3 = (f32[4096]{0:T(1024)S(1)}, f32[4096]{0:T(1024)}, u32[]{:S(2)}) copy-start(f32[4096]{0:T(1024)} %param.9) | copy-start | bytes 49156
  721.1 12.6 %copy-start = (f32[512,4096]{1,0:T(8,128)S(1)}, f32[512,4096]{1,0:T(8,128)}, u32[]{:S(2)}) copy-start(f32[512,4096]{1,0:T(8,128)} %get-tuple-element.6) | copy-start | bytes 25165828
  721.1 12.6 %copy-start.1 = (f32[512,4096]{1,0:T(8,128)S(1)}, f32[512,4096]{1,0:T(8,128)}, u32[]{:S(2)}) copy-start(f32[512,4096]{1,0:T(8,128)} %get-tuple-element.7) | copy-start | bytes 25165828
Sparse Core Ops, SparseCore 0:
  60.7 660.3 all-reduce.2
where the time goes:
time: 765 us; the launch traced here: 764 us
  waiting for transfers between devices  661 us (86%)
  blocking collectives  39.9 us (5%)
  matrix products  32.4 us (4%)
  between operations  14 us (2%)
  local copies, waits for them, and re-layouts  12.6 us (2%)
    psum x1, waiting for transfers between devices, per_device(): preact_sum, code_grad = lax.psum((resid_part, error_part), 'layer')  661 us
    all_gather x1, blocking collectives, per_device(): lax.all_gather(errors, 'feat', axis=0, tiled=True)  21.7 us
    dot_general x2, matrix products, transposed(): lax.dot_general(left, right, (((0,), (0,)), ((), ())), preferred_element_...  19.1 us
    all_gather x1, blocking collectives, per_device(): lax.all_gather(residuals, 'feat', axis=0, tiled=True)  18.2 us
  transfers between devices with their start and end apart: 1, of which 1 were waited for; matrix products, arithmetic and copies ran while one was open for 0% of the time, Pallas kernels for 0%

commit v1 on v0

v1 whole, which is shorter than its diff:
```python
import functools

import jax
import jax.numpy as jnp
from jax import lax
from jax.experimental import pallas as pl
from jax.experimental.pallas import tpu as pltpu
from jax.sharding import PartitionSpec as P

MESH = pl.DeviceIdType.MESH
BF16, F32 = jnp.bfloat16, jnp.float32
CHUNKS = 8
ROWS = 64
HALF = ROWS // 2
STACKED = 512
WIDE, NARROW = 256, 128
SLOTS = ((2, 0), (1, 1), (2, 1), (3, 0), (1, 0), (3, 1), (0, 0), (0, 1))

KINDS = (
    "x1r", "x1l", "x2r", "x2l", "xz", "xgz", "xgr0", "xgl0", "xgr1", "xgl1", "xfr", "xfl",
    "z1", "z1r", "z1l", "z2r", "z2l", "zgr", "zgl", "zfr", "zfl", "zz0", "zz1", "zz3", "zz2",
)


def comm_kernel(
    resid, errors, enc, dec, bias,
    out_resid, out_errors, out_masked, out_code,
    re, xw, zw, xb, zb,
    xp, xr1, xr2, xzr, xo,
    zp, zr1, yr1, yr2, zo,
    send_sem, recv_sem, re_send, re_recv, own_sem, w_sem, out_sem, bias_sem, rout_sem,
):
    here, feat = lax.axis_index("layer"), lax.axis_index("feat")
    x, zh = here // 2, lax.rem(here, 2)
    zl, core = lax.rem(feat // 2, 2), lax.rem(feat, 2)
    right = (lax.rem(here + 2, 8), feat)
    left = (lax.rem(here + 6, 8), feat)
    across = (here + 1 - 2 * zh, feat)
    twin = (here, feat + 1 - 2 * core)
    near = (here, feat + 2 - 4 * zl)
    ups = tuple((here, lax.rem(feat + 4 * k, 16)) for k in (1, 3, 2))

    def x_feats(d, h):
        return pl.multiple_of(lax.rem(x + d, 4) * 512 + lax.rem(zh + h, 2) * 256, 256)

    def z_feats(h, d):
        return pl.multiple_of(2048 + lax.rem(zh + h, 2) * 1024 + lax.rem(x + d, 4) * 256, 256)

    own = [
        pltpu.make_async_copy(src, re.at[m, pl.ds(0, HALF), :], own_sem.at[m])
        for m, src in enumerate((resid, errors))
    ]
    for c in own:
        c.start()
    loads = {}
    for h in (1, 0):
        for d in range(4):
            for m, w in enumerate((enc, dec)):
                loads["z", m, h, d] = pltpu.make_async_copy(
                    w.at[:, pl.ds(z_feats(h, d), WIDE)], zw.at[m, h, d], w_sem.at[m, 8 + h * 4 + d]
                )
    for s, (d, h) in enumerate(SLOTS):
        for m, w in enumerate((enc, dec)):
            loads["x", m, s] = pltpu.make_async_copy(
                w.at[:, pl.ds(x_feats(d, h), WIDE)], xw.at[m, s], w_sem.at[m, s]
            )
    order = (
        [("z", m, 1, d) for d in range(4) for m in range(2)]
        + [("x", m, s) for s in range(8) for m in range(2)]
        + [("z", m, 0, d) for d in range(4) for m in range(2)]
    )
    for key in order:
        loads[key].start()
    biases = [
        pltpu.make_async_copy(bias.at[pl.ds(x_feats(0, 0), WIDE)], xb, bias_sem.at[0]),
        pltpu.make_async_copy(bias.at[pl.ds(z_feats(0, 0), WIDE)], zb, bias_sem.at[1]),
    ]
    for c in biases:
        c.start()

    barrier = pltpu.get_barrier_semaphore()
    friends = (right, left, across, twin, near) + ups
    for friend in friends:
        pl.semaphore_signal(barrier, inc=1, device_id=friend, device_id_type=MESH)
    pl.semaphore_wait(barrier, len(friends))

    def block(c, half):
        return re.at[:, pl.ds(pl.multiple_of(c * ROWS + half * HALF, HALF), HALF), :]

    def re_copy(src, dst, k, target):
        return pltpu.make_async_remote_copy(
            src_ref=block(*src), dst_ref=block(*dst), send_sem=re_send.at[k],
            recv_sem=re_recv.at[dst[0], dst[1]], device_id=target, device_id_type=MESH,
        )

    first = [re_copy((0, 0), (0, 1), 0, twin), re_copy((0, 0), (1, 0), 1, near)]
    first += [re_copy((0, 0), (2 + i, 0), 2 + i, ups[i]) for i in range(3)]
    second = [re_copy((1, 0), (5 + i, 0), 5 + i, ups[i]) for i in range(3)]

    def forward(c):
        return re_copy((c, 0), (c, 1), 7 + c, twin)

    def arrived(c, half):
        re_copy((c, half), (c, half), 0, twin).wait_recv()

    for c in own:
        c.wait()
    for c in first:
        c.start()

    def copy(kind, c):
        k = KINDS.index(kind)
        src, dst, target = {
            "x1r": (xp.at[c, pl.ds(0, 2)], xr1.at[c, 0], right),
            "x1l": (xp.at[c, pl.ds(2, 2)], xr1.at[c, 1], left),
            "x2r": (xp.at[c, 4], xr2.at[c, 0], right),
            "x2l": (xp.at[c, 5], xr2.at[c, 1], left),
            "xz": (xp.at[c, 7], xzr.at[c], across),
            "xgz": (xo.at[c, 0, 0], xo.at[c, 0, 1], across),
            "xgr0": (xo.at[c, 0, 0], xo.at[c, 3, 0], right),
            "xgl0": (xo.at[c, 0, 0], xo.at[c, 1, 0], left),
            "xgr1": (xo.at[c, 0, 1], xo.at[c, 3, 1], right),
            "xgl1": (xo.at[c, 0, 1], xo.at[c, 1, 1], left),
            "xfr": (xo.at[c, 3, 0], xo.at[c, 2, 0], right),
            "xfl": (xo.at[c, 1, 1], xo.at[c, 2, 1], left),
            "z1": (zp.at[c, 1], zr1.at[c], across),
            "z1r": (zp.at[c, 0, pl.ds(0, 2)], yr1.at[c, 0], right),
            "z1l": (zp.at[c, 0, pl.ds(2, 2)], yr1.at[c, 1], left),
            "z2r": (zp.at[c, 0, 4], yr2.at[c, 0], right),
            "z2l": (zp.at[c, 0, 5], yr2.at[c, 1], left),
            "zgr": (zo.at[c, 0, 0], zo.at[c, 0, 3], right),
            "zgl": (zo.at[c, 0, 0], zo.at[c, 0, 1], left),
            "zfr": (zo.at[c, 0, 3, 0], zo.at[c, 0, 2, 0], right),
            "zfl": (zo.at[c, 0, 1, 1], zo.at[c, 0, 2, 1], left),
            "zz0": (zo.at[c, 0, 0], zo.at[c, 1, 0], across),
            "zz1": (zo.at[c, 0, 1], zo.at[c, 1, 1], across),
            "zz3": (zo.at[c, 0, 3], zo.at[c, 1, 3], across),
            "zz2": (zo.at[c, 0, 2], zo.at[c, 1, 2], across),
        }[kind]
        return pltpu.make_async_remote_copy(
            src_ref=src, dst_ref=dst, send_sem=send_sem.at[k], recv_sem=recv_sem.at[k, c],
            device_id=target, device_id_type=MESH,
        )

    def start(kind, c):
        @pl.when(c > 0)
        def _():
            copy(kind, c - 1).wait_send()

        copy(kind, c).start()

    def got(kind, c):
        copy(kind, c).wait_recv()

    def dot(m, rows, w):
        return jnp.dot(rows[m], w[...], preferred_element_type=F32).astype(BF16)

    def stage0(c):
        @pl.when(c == 0)
        def _():
            arrived(0, 1)
            arrived(1, 0)
            for cc in second:
                cc.start()

        @pl.when(c > 0)
        def _():
            arrived(c, 1)

            @pl.when(c < CHUNKS - 1)
            def _():
                arrived(c + 1, 0)

        @pl.when(c < CHUNKS - 1)
        def _():
            forward(c + 1).start()

        at = pl.ds(pl.multiple_of(c * ROWS, ROWS), ROWS)
        rows = (re[0, at, :], re[1, at, :])

        def ready(*key):
            @pl.when(c == 0)
            def _():
                loads[key].wait()

        def z_part(h):
            for d in range(4):
                for m in range(2):
                    ready("z", m, h, d)
                    got_ = dot(m, rows, zw.at[m, h, d])
                    for half in range(2):
                        zp[c, h, SLOTS.index((d, half)), m] = got_[:, half * NARROW:(half + 1) * NARROW]

        def x_part(slots):
            for s in slots:
                for m in range(2):
                    ready("x", m, s)
                    xp[c, s, m] = dot(m, rows, xw.at[m, s])

        z_part(1)
        start("z1", c)
        x_part((0, 1))
        start("x1r", c)
        x_part((2, 3))
        start("x1l", c)
        x_part((4, 5, 6, 7))
        z_part(0)

    def add(*parts):
        total = parts[0].astype(F32)
        for p in parts[1:]:
            total += p.astype(F32)
        return total

    def stage1(c):
        got("x1r", c)
        xp[c, 4] = add(xp[c, 4], xr1[c, 0, 0]).astype(BF16)
        start("x2r", c)
        got("x1l", c)
        xp[c, 5] = add(xp[c, 5], xr1[c, 1, 0]).astype(BF16)
        start("x2l", c)
        got("z1", c)
        for s in (0, 1):
            zp[c, 0, s] = add(zp[c, 0, s], zr1[c, s]).astype(BF16)
        start("z1r", c)
        for s in (2, 3):
            zp[c, 0, s] = add(zp[c, 0, s], zr1[c, s]).astype(BF16)
        start("z1l", c)

    def stage2(c):
        got("x2l", c)
        xp[c, 7] = add(xp[c, 7], xr2[c, 1], xr1[c, 0, 1]).astype(BF16)
        start("xz", c)
        got("z1r", c)
        zp[c, 0, 4] = add(zp[c, 0, 4], zr1[c, 4], yr1[c, 0, 0]).astype(BF16)
        start("z2r", c)
        got("z1l", c)
        zp[c, 0, 5] = add(zp[c, 0, 5], zr1[c, 5], yr1[c, 1, 0]).astype(BF16)
        start("z2l", c)

    def gate(total, b):
        pre = 4.0 * (total[0] + b[None, :])
        e = jnp.exp(-jnp.abs(pre))
        code = (jnp.maximum(pre, 0.0) + jnp.log1p(e)) * 0.25
        masked = total[1] * (jnp.where(pre >= 0, 1.0, e) / (1.0 + e))
        return masked.astype(BF16), code.astype(BF16)

    def stage3(c):
        got("x2r", c)
        got("xz", c)
        masked, code = gate(add(xp[c, 6], xr2[c, 0], xr1[c, 1, 1], xzr[c]), xb[...])
        xo[c, 0, 0, 0] = masked
        xo[c, 0, 0, 1] = code
        start("xgz", c)
        start("xgr0", c)
        start("xgl0", c)
        got("z2r", c)
        got("z2l", c)
        for half in range(2):
            total = add(zp[c, 0, 6 + half], zr1[c, 6 + half], yr2[c, half], yr1[c, 1 - half, 1])
            masked, code = gate(total, zb[pl.ds(half * NARROW, NARROW)])
            zo[c, 0, 0, half, 0] = masked
            zo[c, 0, 0, half, 1] = code
        start("zgr", c)
        start("zgl", c)
        start("zz0", c)

    def stage4(c):
        got("xgz", c)
        start("xgr1", c)
        start("xgl1", c)
        got("xgr0", c)
        start("xfr", c)
        got("zgr", c)
        start("zfr", c)
        start("zz3", c)
        got("zgl", c)
        start("zfl", c)
        start("zz1", c)

    def stage5(c):
        got("xgl1", c)
        start("xfl", c)
        got("zfr", c)
        got("zfl", c)
        start("zz2", c)

    def stores(c):
        at = pl.ds(pl.multiple_of(c * ROWS, ROWS), ROWS)
        found = []
        for m, out in enumerate((out_masked, out_code)):
            for d in range(4):
                for h in range(2):
                    found.append((xo.at[c, d, h, m], out.at[at, pl.ds(x_feats(d, h), WIDE)]))
                    for half in range(2):
                        found.append((
                            zo.at[c, h, d, half, m],
                            out.at[at, pl.ds(pl.multiple_of(z_feats(h, d) + half * NARROW, NARROW), NARROW)],
                        ))
        return [pltpu.make_async_copy(a, b, out_sem.at[i]) for i, (a, b) in enumerate(found)]

    def stage6(c):
        for kind in ("xgl0", "xgr1", "xfr", "xfl", "zz0", "zz1", "zz3", "zz2"):
            got(kind, c)

        @pl.when(c > 0)
        def _():
            for cc in stores(c - 1):
                cc.wait()

        for cc in stores(c):
            cc.start()

    for c in biases:
        c.wait()

    def step(i, carry):
        for lag, stage in enumerate((stage0, stage1, stage2, stage3, stage4, stage5, stage6)):
            @pl.when((i >= lag) & (i < lag + CHUNKS))
            def _():
                stage(i - lag)

        return carry

    lax.fori_loop(0, CHUNKS + 6, step, 0)

    rout = [
        pltpu.make_async_copy(re.at[m], out, rout_sem.at[m]) for m, out in enumerate((out_resid, out_errors))
    ]
    for c in rout:
        c.start()
    for kind in KINDS:
        copy(kind, CHUNKS - 1).wait_send()
    for c in first + second + [forward(k) for k in range(1, CHUNKS)]:
        c.wait_send()
    for c in rout + stores(CHUNKS - 1):
        c.wait()


def gathered(residuals, errors, enc_weight, dec_weight, enc_bias):
    feats = enc_weight.shape[1]
    tokens = CHUNKS * ROWS
    dma, any_ = pltpu.SemaphoreType.DMA, pl.BlockSpec(memory_space=pl.ANY)
    return pl.pallas_call(
        comm_kernel,
        out_shape=[
            jax.ShapeDtypeStruct((tokens, STACKED), BF16),
            jax.ShapeDtypeStruct((tokens, STACKED), BF16),
            jax.ShapeDtypeStruct((tokens, feats), BF16),
            jax.ShapeDtypeStruct((tokens, feats), BF16),
        ],
        in_specs=[any_] * 5,
        out_specs=[any_] * 4,
        scratch_shapes=[
            pltpu.VMEM((2, tokens, STACKED), BF16),
            pltpu.VMEM((2, 8, STACKED, WIDE), BF16),
            pltpu.VMEM((2, 2, 4, STACKED, WIDE), BF16),
            pltpu.VMEM((WIDE,), F32),
            pltpu.VMEM((WIDE,), F32),
            pltpu.VMEM((CHUNKS, 8, 2, ROWS, WIDE), BF16),
            pltpu.VMEM((CHUNKS, 2, 2, 2, ROWS, WIDE), BF16),
            pltpu.VMEM((CHUNKS, 2, 2, ROWS, WIDE), BF16),
            pltpu.VMEM((CHUNKS, 2, ROWS, WIDE), BF16),
            pltpu.VMEM((CHUNKS, 4, 2, 2, ROWS, WIDE), BF16),
            pltpu.VMEM((CHUNKS, 2, 8, 2, ROWS, NARROW), BF16),
            pltpu.VMEM((CHUNKS, 8, 2, ROWS, NARROW), BF16),
            pltpu.VMEM((CHUNKS, 2, 2, 2, ROWS, NARROW), BF16),
            pltpu.VMEM((CHUNKS, 2, 2, ROWS, NARROW), BF16),
            pltpu.VMEM((CHUNKS, 2, 4, 2, 2, ROWS, NARROW), BF16),
            dma((len(KINDS),)),
            dma((len(KINDS), CHUNKS)),
            dma((15,)),
            dma((CHUNKS, 2)),
            dma((2,)),
            dma((2, 16)),
            dma((48,)),
            dma((2,)),
            dma((2,)),
        ],
        compiler_params=pltpu.CompilerParams(
            collective_id=0, has_side_effects=True, vmem_limit_bytes=60 * 2**20
        ),
    )(residuals, errors, enc_weight, dec_weight, enc_bias)


def transposed(left, right):
    return lax.dot_general(left, right, (((0,), (0,)), ((), ())), preferred_element_type=F32)


def per_device(residuals, errors, enc_weight, dec_weight, enc_bias):
    all_resid, all_errors, masked, code = gathered(residuals, errors, enc_weight, dec_weight, enc_bias)
    enc_grad = transposed(all_resid, masked)
    dec_grad = transposed(all_errors, code)
    bias_grad = jnp.sum(masked.astype(F32), axis=0)
    return enc_grad.astype(BF16), dec_grad.astype(BF16), bias_grad


def solution(mesh):
    placed = (P("feat", "layer"), P("feat", "layer"), P("layer", "feat"), P("layer", "feat"), P("feat"))
    return jax.shard_map(
        per_device,
        mesh=mesh,
        in_specs=placed,
        out_specs=(P("layer", "feat"), P("layer", "feat"), P("feat")),
        check_vma=False,
    )
```

time: 765 us -> 148 us (0.19)
  waiting for transfers between devices: 661 us -> 0 us
  Pallas kernels: 0 us -> 131 us
  blocking collectives: 39.9 us -> 0 us
  matrix products: 32.4 us -> 9.96 us
  between operations: 14 us -> 0.65 us
  local copies, waits for them, and re-layouts: 12.6 us -> 0.01 us
    psum x1 -> x0, waiting for transfers between devices: 661 us -> none  [per_device(): preact_sum, code_grad = lax.psum((resid_part, error_part), 'layer')]
    pallas_call x0 -> x1, Pallas kernels: none -> 131 us  [gathered(): pl.pallas_call(comm_kernel, out_shape=[jax.ShapeDtypeStruct((tokens, STAC...]
    all_gather x2 -> x0, blocking collectives: 39.9 us -> none  [the longest x1 21.7 us: per_device(): lax.all_gather(errors, 'feat', axis=0, tiled=True)]
    dot_general x2 -> x0, matrix products: 13.4 us -> none  [the longest x1 7.75 us: per_device(): jnp.dot(all_errors, dec_weight, preferred_element_type=jnp.float32)]
    unnamed x10 -> x6, local copies, waits for them, and re-layouts: 12.6 us -> 0.01 us
    dot_general x2, matrix products: 19.1 us -> 9.96 us  [transposed(): lax.dot_general(left, right, (((0,), (0,)), ((), ())), preferred_element_...]
  transfers between devices with their start and end apart: 1 -> 0, of which waited for: 1 -> 0; matrix products, arithmetic and copies ran while one was open for 0% -> 0% of each run, Pallas kernels for 0% -> 0%
where the time goes in v1:
time: 148 us; the launch traced here: 145 us
  Pallas kernels  131 us (89%)
  matrix products  9.96 us (7%)
  other arithmetic  3.92 us (3%)
    pallas_call x1, Pallas kernels, gathered(): pl.pallas_call(comm_kernel, out_shape=[jax.ShapeDtypeStruct((tokens, STAC...  131 us
    dot_general x2, matrix products, transposed(): lax.dot_general(left, right, (((0,), (0,)), ((), ())), preferred_element_...  9.96 us
    reduce_sum x1, other arithmetic, per_device(): bias_grad = jnp.sum(masked.astype(F32), axis=0)  3.92 us

profile of v1, /device:TPU:36, one launch (start us, length us, event | category | flops | bytes accessed | tf_op | source)
XLA Modules:
  0.0 145.3 jit_solution(3134088186343337757)
XLA Ops:
  0.6 130.7 %shard_map.76 = (bf16[512,512]{1,0:T(8,128)(2,1)}, bf16[512,512]{1,0:T(8,128)(2,1)}, bf16[512,4096]{1,0:T(8,128)(2,1)}, bf16[512,4096]{1,0:T(8,128)(2,1)}) custom-call(bf16[32,512]{1,0:T(8,128)(2,1)} %resid.1, bf16[32,512]{1,0:T(8,128)(2,1)} %errors.1, bf16[512,4096]{1,0:T(8,128)(2,1)} %enc.1, bf16[512,4096]{1,0:T(8,128)(2,1)} %dec.1, f32[4096]{0:T(1024)} %bias.1), custom_call_target="tpu_custom_call" | custom-call | tf_op jit(solution)/shard_map/pallas_call | solution.py:344
  131.4 0.0 copy-start
  131.4 3.9 %convert_reduce_fusion = f32[4096]{0:T(1024)} fusion(bf16[512,4096]{1,0:T(8,128)(2,1)} %get-tuple-element.8), kind=kLoop, calls=%fused_computation | loop fusion | flops 4190208 | bytes 4210688 | tf_op jit(solution)/shard_map/reduce_sum | solution.py:394
  135.3 0.0 copy-done
  135.3 0.0 copy-start.1
  135.3 0.0 copy-start.2
  135.3 5.6 %convolution_convert_fusion.1 = bf16[512,4096]{1,0:T(8,128)(2,1)} fusion(bf16[512,512]{1,0:T(8,128)(2,1)} %get-tuple-element.7, bf16[512,4096]{1,0:T(8,128)(2,1)S(1)} %copy-done), kind=kOutput, calls=%fused_computation.2 | convolution fusion | flops 2149580800 | bytes 8912896 | tf_op jit(solution)/shard_map/dot_general | solution.py:387
  140.9 0.0 copy-done.1
  140.9 0.0 copy-done.2
  140.9 4.4 %convolution_convert_fusion = bf16[512,4096]{1,0:T(8,128)(2,1)} fusion(bf16[512,512]{1,0:T(8,128)(2,1)S(1)} %copy-done.2, bf16[512,4096]{1,0:T(8,128)(2,1)S(1)} %copy-done.1), kind=kOutput, calls=%fused_computation.1 | convolution fusion | flops 2149580800 | bytes 8912896 | tf_op jit(solution)/shard_map/dot_general | solution.py:387
Async XLA Ops:
  131.4 3.9 %copy-start = (bf16[512,4096]{1,0:T(8,128)(2,1)S(1)}, bf16[512,4096]{1,0:T(8,128)(2,1)}, u32[]{:S(2)}) copy-start(bf16[512,4096]{1,0:T(8,128)(2,1)} %get-tuple-element.8) | copy-start | bytes 12582916
  135.3 5.6 %copy-start.1 = (bf16[512,4096]{1,0:T(8,128)(2,1)S(1)}, bf16[512,4096]{1,0:T(8,128)(2,1)}, u32[]{:S(2)}) copy-start(bf16[512,4096]{1,0:T(8,128)(2,1)} %get-tuple-element.10) | copy-start | bytes 12582916
  135.3 5.6 %copy-start.2 = (bf16[512,512]{1,0:T(8,128)(2,1)S(1)}, bf16[512,512]{1,0:T(8,128)(2,1)}, u32[]{:S(2)}) copy-start(bf16[512,512]{1,0:T(8,128)(2,1)} %get-tuple-element.9) | copy-start | bytes 1572868
